TPU v7x, 512 devices: a whole 4x4x16 slice. The times are simulated.
512 devices in a mesh: dp: 64 (over z, y_lo, core), tensor: 8 (over x, y_hi).
Axes of the slice: x: 4, y: 4 (y_hi: 2, y_lo: 2; y = y_hi * 2 + y_lo), z: 16, core: 2. Of those that a mesh axis runs over, the one named last changes fastest.
Arguments:
- activations: bfloat16 [131072, 1024], P(('dp', 'tensor')), may hold values from -24 to 24
- gradients: bfloat16 [131072, 5472], P('dp', 'tensor'), may hold values from -6 to 6
- act_history: float32 [8, 16, 1024], P('tensor'), may hold values from 0.1 to 4
- grad_history: float32 [16, 5472], P(None, 'tensor'), may hold values from 0.1 to 4
- owner_rank: int32 [1024], replicated, may hold values from 0 to 7
- history_slot: int32 [6496], replicated, may hold values from 0 to 15
Outputs:
- weight_grad: float32 [1024, 5472], P('dp', 'tensor')
- act_history_out: float32 [8, 16, 1024], P('tensor')
- grad_history_out: float32 [16, 5472], P(None, 'tensor')
All inputs are finite; a program needn't handle non-finite values.
Results may differ from a plain program's by a relative error of at most 0.0042.
Values may be sent and summed in bfloat16 or wider, within the bound.
A program may use at most 64 MiB of HBM per device.

v0:
```python
import math
import jax
import jax.numpy as jnp
from jax import lax
from jax.sharding import PartitionSpec as P

QUANT_LIMIT = 448.0
SCALE_FLOOR = 0.25


def sent_to_all(value, axis):
    copies = jnp.broadcast_to(value, (lax.axis_size(axis), *value.shape))
    return lax.all_to_all(copies, axis, split_axis=0, concat_axis=0, tiled=True)


def of_everyone(value, axis):
    everything = sent_to_all(value, axis)
    return jnp.sum(everything, axis=0)


def cut_along(value, dim, length):
    lengths = value.shape
    parts = value.reshape(*lengths[:dim], length, lengths[dim] // length, *lengths[dim + 1 :])
    return jnp.moveaxis(parts, dim, 0)


def summed_on_arrival(value, axis, dim):
    length = lax.axis_size(axis)
    parts = lax.all_to_all(cut_along(value, dim, length), axis, 0, 0, tiled=True)
    return jnp.sum(parts.astype(jnp.float32), axis=0)


def taken_together(value, axis):
    everything = sent_to_all(value, axis)
    return jnp.max(everything, axis=0)


def in_one(arrays, axis):
    flat, at, done = (jnp.concatenate([a.reshape(-1) for a in arrays]), 0, [])
    subtotal = taken_together(flat, axis)
    for a in arrays:
        done.append(subtotal[at : at + a.size].reshape(a.shape))
        at += a.size
    return tuple(done)


def quantize(values, scale):
    scaled = values.astype(jnp.float32) * scale
    return jnp.clip(scaled, -QUANT_LIMIT, QUANT_LIMIT).astype(jnp.bfloat16)


def place_peaks(history, peaks, slots):
    rows = lax.broadcasted_iota(jnp.int32, history.shape, 0)
    return jnp.where(rows == slots[None, :], peaks[None, :], history)


def body(activations, gradients, act_history, grad_history, owner_rank, history_slot):
    model_width = act_history.shape[2]
    column_total = gradients.shape[1]
    my_rank = lax.axis_index("tensor")
    held = jnp.where(owner_rank[None, :] == my_rank, act_history[0], jnp.float32(0.0))
    current_history = of_everyone(held, "tensor")
    act_scale = QUANT_LIMIT / jnp.maximum(jnp.max(current_history, axis=0), SCALE_FLOOR)
    grad_scale = QUANT_LIMIT / jnp.maximum(jnp.max(grad_history, axis=0), SCALE_FLOOR)
    grad_quant = quantize(gradients, grad_scale)
    row_count = model_width // lax.axis_size("dp")
    grad_factor = 1.0 / math.sqrt(gradients.shape[0] * lax.axis_size("dp"))
    own_grad_peak = jnp.max(jnp.abs(gradients), axis=0).astype(jnp.float32)
    contract_rows = (((0,), (0,)), ((), ()))
    gathered_peak = jnp.zeros((model_width,), jnp.float32)
    act_piece = lax.all_gather(activations, "tensor", axis=0, tiled=True)
    running_peak = gathered_peak
    quantized = quantize(act_piece, act_scale)
    peak_next = jnp.maximum(running_peak, jnp.max(jnp.abs(act_piece), axis=0).astype(jnp.float32))
    partial_sum = lax.dot_general(
        quantized, grad_quant, contract_rows, preferred_element_type=jnp.float32
    )
    partial_sum, gathered_peak = (partial_sum, peak_next)
    summed = summed_on_arrival(partial_sum.astype(jnp.bfloat16), "dp", 0)
    act_peak, grad_peak = in_one((gathered_peak, own_grad_peak), "dp")
    row_base = lax.axis_index("dp") * row_count
    row_scale = lax.dynamic_slice_in_dim(act_scale, row_base, row_count, 0)
    weight_grad = summed / (row_scale[:, None] * grad_scale[None, :]) * grad_factor
    act_slots = history_slot[:model_width]
    grad_slots = lax.dynamic_slice_in_dim(
        history_slot, model_width + my_rank * column_total, column_total, 0
    )
    updated = place_peaks(current_history, act_peak, act_slots)
    act_history_out = updated[None]
    grad_history_out = place_peaks(grad_history, grad_peak, grad_slots)
    return (weight_grad, act_history_out, grad_history_out)


def solution(mesh):
    placed = (
        P(("dp", "tensor"), None),
        P("dp", "tensor"),
        P("tensor", None, None),
        P(None, "tensor"),
        P(),
        P(),
    )
    return jax.shard_map(
        body,
        mesh=mesh,
        in_specs=placed,
        out_specs=(P("dp", "tensor"), P("tensor", None, None), P(None, "tensor")),
        check_vma=False,
    )
```

profile of v0, /device:TPU:8, one launch (start us, length us, event | category | flops | bytes accessed | tf_op | source)
XLA Modules:
  0.0 252.6 jit_solution(7629873349470279669)
XLA Ops:
  7.2 0.0 all-gather.2.cloned.1.call-start
  7.2 0.7 all-gather.2.cloned.1.call-update
  7.9 0.7 broadcast_compare_fusion
  8.6 0.8 bitcast_select_fusion.1
  9.4 0.8 broadcast_in_dim.49
  10.3 6.0 %all-to-all-start = ((f32[8,16,1024]{2,1,0:T(8,128)}), f32[8,16,1024]{2,1,0:T(8,128)S(1)}, u32[]{:S(2)}, u32[]{:S(2)}) async-start(f32[8,16,1024]{2,1,0:T(8,128)} %broadcast_in_dim.49), calls=%async_computation | async-start | bytes 1048576 | tf_op jit(solution)/shard_map/all_to_all | solution.py:13
  16.3 0.0 copy-start.2
  16.3 0.0 copy-start.1
  16.3 0.0 copy-start
  16.3 2.6 %abs_reduce_fusion.1 = bf16[684]{0:T(1024)(128)(2,1)S(1)} fusion(bf16[2048,684]{0,1:T(8,128)(2,1)} %param.7), kind=kLoop, calls=%fused_computation.8 | loop fusion | flops 2800980 | bytes 2803032 | tf_op jit(solution)/shard_map/reduce_max | solution.py:68
  18.9 82.8 %all-gather.2.cloned.1.call-done = bf16[2048,1024]{1,0:T(8,128)(2,1)} async-done(((bf16[256,1024]{1,0:T(8,128)(2,1)}), bf16[2048,1024]{1,0:T(8,128)(2,1)}) %all-gather.2.cloned.1.call-update) | async-done | bytes 4194320 | tf_op jit(solution)/shard_map/all_gather | solution.py:71
  101.7 2.6 %abs_reduce_fusion = bf16[1024]{0:T(1024)(128)(2,1)S(1)} fusion(bf16[2048,1024]{1,0:T(8,128)(2,1)} %all-gather.2.cloned.1.call-done), kind=kLoop, calls=%fused_computation.3 | loop fusion | flops 4193280 | bytes 4196352 | tf_op jit(solution)/shard_map/reduce_max | solution.py:74
  104.3 0.0 all-to-all-done
  104.4 1.0 broadcast_in_dim.51
  105.4 14.4 %all-to-all-start.2 = ((f32[64,1,1708]{2,1,0:T(1,128)}), f32[64,1,1708]{2,1,0:T(1,128)}, u32[]{:S(2)}, u32[]{:S(2)}) async-start(f32[64,1,1708]{2,1,0:T(1,128)} %broadcast_in_dim.51), calls=%async_computation.2 | async-start | bytes 917504 | tf_op jit(solution)/shard_map/all_to_all | solution.py:13
  119.8 0.0 copy-done.2
  119.8 0.1 dynamic_slice.7
  119.9 30.5 %all-to-all-done.2 = f32[64,1,1708]{2,1,0:T(1,128)} async-done(((f32[64,1,1708]{2,1,0:T(1,128)}), f32[64,1,1708]{2,1,0:T(1,128)}, u32[]{:S(2)}, u32[]{:S(2)}) %all-to-all-start.2) | async-done | bytes 437280 | tf_op jit(solution)/shard_map/all_to_all | solution.py:13
  150.4 1.3 reduce_max.49
  151.8 0.0 copy-done.1
  151.8 0.6 fusion.8
  152.4 0.0 copy-done
  152.4 6.5 %fusion.7 = bf16[1024,684]{0,1:T(8,128)(2,1)} fusion(bf16[2048,684]{0,1:T(8,128)(2,1)S(1)} %copy-done, f32[684]{0:T(1024)S(1)} %maximum_divide_fusion, bf16[2048,1024]{1,0:T(8,128)(2,1)} %all-gather.2.cloned.1.call-done, f32[1024]{0:T(1024)S(1)} %maximum_divide_fusion.1), kind=kOutput, calls=%fused_computation.12 | convolution fusion | flops 2883596288 | bytes 8403632 | tf_op jit(solution)/shard_map/dot_general | solution.py:75
  158.9 0.0 slice-start
  158.9 2.6 %copy.11 = bf16[1024,684]{1,0:T(8,128)(2,1)} copy(bf16[1024,684]{0,1:T(8,128)(2,1)} %fusion.7) | data formatting | bytes 2801664 | tf_op jit(solution)/shard_map/convert_element_type | solution.py:79
  161.5 4.7 %all-to-all-start.1 = ((bf16[64,16,684]{2,1,0:T(8,128)(2,1)}), bf16[64,16,684]{2,1,0:T(8,128)(2,1)S(1)}, u32[]{:S(2)}, u32[]{:S(2)}) async-start(bf16[64,16,684]{2,1,0:T(8,128)(2,1)} %bitcast.1), calls=%async_computation.1 | async-start | bytes 3145728 | tf_op jit(solution)/shard_map/all_to_all | solution.py:29
  166.2 0.1 dynamic_slice.6
  166.3 0.0 slice-done
  166.3 0.6 bitcast_select_fusion
  166.9 77.9 %all-to-all-done.1 = bf16[64,16,684]{2,1,0:T(8,128)(2,1)S(1)} async-done(((bf16[64,16,684]{2,1,0:T(8,128)(2,1)}), bf16[64,16,684]{2,1,0:T(8,128)(2,1)S(1)}, u32[]{:S(2)}, u32[]{:S(2)}) %all-to-all-start.1) | async-done | bytes 1400864 | tf_op jit(solution)/shard_map/all_to_all | solution.py:29
  244.8 0.3 convert_reduce_fusion
  245.1 0.7 divide_multiply_fusion
  (9 shorter events, 0.1 us)
Async XLA Ops:
  7.2 94.5 %all-gather.2.cloned.1.call-start = ((), (), s32[]{:S(2)}) async-start(), calls=%async_computation.3 | async-start | bytes 4718592 | tf_op jit(solution)/shard_map/all_gather | solution.py:71
  10.3 94.1 %all-to-all-start = ((f32[8,16,1024]{2,1,0:T(8,128)}), f32[8,16,1024]{2,1,0:T(8,128)S(1)}, u32[]{:S(2)}, u32[]{:S(2)}) async-start(f32[8,16,1024]{2,1,0:T(8,128)} %broadcast_in_dim.49), calls=%async_computation | async-start | bytes 1048576 | tf_op jit(solution)/shard_map/all_to_all | solution.py:13
  16.3 103.4 %copy-start.2 = (s32[6496]{0:T(1024)S(1)}, s32[6496]{0:T(1024)}, u32[]{:S(2)}) copy-start(s32[6496]{0:T(1024)} %param.11) | copy-start | bytes 77956
  16.3 135.4 %copy-start.1 = (f32[16,684]{1,0:T(8,128)S(1)}, f32[16,684]{1,0:T(8,128)}, u32[]{:S(2)}) copy-start(f32[16,684]{1,0:T(8,128)} %param.9) | copy-start | bytes 131332
  16.3 136.1 %copy-start = (bf16[2048,684]{0,1:T(8,128)(2,1)S(1)}, bf16[2048,684]{0,1:T(8,128)(2,1)}, u32[]{:S(2)}) copy-start(bf16[2048,684]{0,1:T(8,128)(2,1)} %param.7) | copy-start | bytes 8404996
  105.4 45.1 %all-to-all-start.2 = ((f32[64,1,1708]{2,1,0:T(1,128)}), f32[64,1,1708]{2,1,0:T(1,128)}, u32[]{:S(2)}, u32[]{:S(2)}) async-start(f32[64,1,1708]{2,1,0:T(1,128)} %broadcast_in_dim.51), calls=%async_computation.2 | async-start | bytes 917504 | tf_op jit(solution)/shard_map/all_to_all | solution.py:13
  158.9 7.4 %slice-start = ((s32[6496]{0:T(1024)}), s32[1024]{0:T(1024)S(1)}, s32[]{:S(2)}) async-start(s32[6496]{0:T(1024)} %param.11), calls=%async_computation.4 | async-start | bytes 8192 | tf_op jit(solution)/shard_map/slice | solution.py:84
  161.5 83.3 %all-to-all-start.1 = ((bf16[64,16,684]{2,1,0:T(8,128)(2,1)}), bf16[64,16,684]{2,1,0:T(8,128)(2,1)S(1)}, u32[]{:S(2)}, u32[]{:S(2)}) async-start(bf16[64,16,684]{2,1,0:T(8,128)(2,1)} %bitcast.1), calls=%async_computation.1 | async-start | bytes 3145728 | tf_op jit(solution)/shard_map/all_to_all | solution.py:29
Sparse Core Ops, SparseCore 0:
  11.2 90.4 all-gather.1
where the time goes:
time: 253 us
  waiting for transfers between devices  192 us (76%)
  starting transfers between devices  25.1 us (10%)
  between operations  14.1 us (6%)
  other arithmetic  10.3 us (4%)
  matrix products  6.51 us (3%)
  local copies, waits for them, and re-layouts  4.63 us (2%)
    all_gather x1, waiting for transfers between devices, body(): act_piece = lax.all_gather(activations, 'tensor', axis=0, tiled=True)  82.8 us
    all_to_all x1, waiting for transfers between devices, summed_on_arrival(): lax.all_to_all(cut_along(value, dim, length), axis, 0, 0, tiled=True)  77.9 us
    all_to_all x2, waiting for transfers between devices, sent_to_all(): return lax.all_to_all(copies, axis, split_axis=0, concat_axis=0, tiled=True)  30.5 us
    all_to_all x2, starting transfers between devices, sent_to_all(): return lax.all_to_all(copies, axis, split_axis=0, concat_axis=0, tiled=True)  20.4 us
    dot_general x1, matrix products, body(): lax.dot_general(quantized, grad_quant, contract_rows, preferred_element_t...  6.51 us
  transfers between devices with their start and end apart: 4, of which 3 were waited for; matrix products, arithmetic and copies ran while one was open for 3% of the time, Pallas kernels for 0%

commit v1 on v0

--- a/solution.py
+++ b/solution.py
@@ -68,7 +68,8 @@
     own_grad_peak = jnp.max(jnp.abs(gradients), axis=0).astype(jnp.float32)
     contract_rows = (((0,), (0,)), ((), ()))
     gathered_peak = jnp.zeros((model_width,), jnp.float32)
-    act_piece = lax.all_gather(activations, "tensor", axis=0, tiled=True)
+    sent = jnp.stack([activations] * lax.axis_size("tensor"))
+    act_piece = jnp.concatenate(lax.all_to_all(sent, "tensor", 0, 0), axis=0)
     running_peak = gathered_peak
     quantized = quantize(act_piece, act_scale)
     peak_next = jnp.maximum(running_peak, jnp.max(jnp.abs(act_piece), axis=0).astype(jnp.float32))

time: 253 us -> 231 us (0.913)
  waiting for transfers between devices: 192 us -> 175 us
  between operations: 14.1 us -> 0.76 us
  starting transfers between devices: 25.1 us -> 33.3 us
  local copies, waits for them, and re-layouts: 4.63 us -> 8.19 us
  other arithmetic: 10.3 us -> 6.86 us
    all_gather x1 -> x0, waiting for transfers between devices: 82.8 us -> none  [body(): act_piece = lax.all_gather(activations, 'tensor', axis=0, tiled=True)]
    all_to_all x0 -> x1, waiting for transfers between devices: none -> 58.9 us  [body(): act_piece = jnp.concatenate(lax.all_to_all(sent, 'tensor', 0, 0), axis=0)]
    all_to_all x2, waiting for transfers between devices: 30.5 us -> 38 us  [sent_to_all(): return lax.all_to_all(copies, axis, split_axis=0, concat_axis=0, tiled=True)]
    all_to_all x0 -> x1, starting transfers between devices: none -> 6.29 us  [body(): act_piece = jnp.concatenate(lax.all_to_all(sent, 'tensor', 0, 0), axis=0)]
    another operation x0 -> x1, local copies, waits for them, and re-layouts: none -> 3.55 us  [body(): sent = jnp.stack([activations] * lax.axis_size('tensor'))]
  transfers between devices with their start and end apart: 4 -> 4, of which waited for: 3 -> 4; matrix products, arithmetic and copies ran while one was open for 3% -> 2% of each run, Pallas kernels for 0% -> 0%
where the time goes in v1:
time: 231 us; the launch traced here: 230 us
  waiting for transfers between devices  175 us (76%)
  starting transfers between devices  33.3 us (14%)
  local copies, waits for them, and re-layouts  8.19 us (4%)
  other arithmetic  6.86 us (3%)
  matrix products  6.5 us (3%)
    all_to_all x1, waiting for transfers between devices, summed_on_arrival(): lax.all_to_all(cut_along(value, dim, length), axis, 0, 0, tiled=True)  77.9 us
    all_to_all x1, waiting for transfers between devices, body(): act_piece = jnp.concatenate(lax.all_to_all(sent, 'tensor', 0, 0), axis=0)  58.9 us
    all_to_all x2, waiting for transfers between devices, sent_to_all(): return lax.all_to_all(copies, axis, split_axis=0, concat_axis=0, tiled=True)  38 us
    all_to_all x2, starting transfers between devices, sent_to_all(): return lax.all_to_all(copies, axis, split_axis=0, concat_axis=0, tiled=True)  22.3 us
    dot_general x1, matrix products, body(): lax.dot_general(quantized, grad_quant, contract_rows, preferred_element_t...  6.5 us
    all_to_all x1, starting transfers between devices, body(): act_piece = jnp.concatenate(lax.all_to_all(sent, 'tensor', 0, 0), axis=0)  6.29 us
    all_to_all x1, starting transfers between devices, summed_on_arrival(): lax.all_to_all(cut_along(value, dim, length), axis, 0, 0, tiled=True)  4.69 us
  transfers between devices with their start and end apart: 4, of which 4 were waited for; matrix products, arithmetic and copies ran while one was open for 2% of the time, Pallas kernels for 0%

profile of v1, /device:TPU:8, one launch (start us, length us, event | category | flops | bytes accessed | tf_op | source)
XLA Modules:
  0.0 230.4 jit_solution(12907136774859733343)
XLA Ops:
  0.6 3.5 %stack.2 = bf16[8,256,1024]{2,1,0:T(8,128)(2,1)} broadcast(bf16[256,1024]{1,0:T(8,128)(2,1)} %param.6), dimensions={1,2} | broadcast | bytes 4718592 | tf_op jit(solution)/shard_map/stack | solution.py:71
  4.2 0.0 copy-start
  4.2 0.0 copy-start.4
  4.2 0.0 copy-start.1
  4.2 6.3 %all-to-all-start = ((bf16[8,256,1024]{2,1,0:T(8,128)(2,1)}), bf16[8,256,1024]{2,1,0:T(8,128)(2,1)}, u32[]{:S(2)}, u32[]{:S(2)}) async-start(bf16[8,256,1024]{2,1,0:T(8,128)(2,1)} %stack.2), calls=%async_computation | async-start | bytes 8388608 | tf_op jit(solution)/shard_map/all_to_all | solution.py:72
  10.5 0.0 copy-done
  10.5 0.6 abs_reduce_fusion.1
  11.1 0.0 copy-done.4
  11.1 0.0 copy-done.1
  11.2 0.0 copy-start.2
  11.2 58.9 %all-to-all-done = bf16[8,256,1024]{2,1,0:T(8,128)(2,1)} async-done(((bf16[8,256,1024]{2,1,0:T(8,128)(2,1)}), bf16[8,256,1024]{2,1,0:T(8,128)(2,1)}, u32[]{:S(2)}, u32[]{:S(2)}) %all-to-all-start) | async-done | bytes 4194336 | tf_op jit(solution)/shard_map/all_to_all | solution.py:72
  70.1 0.8 broadcast_in_dim.49
  70.9 5.0 %all-to-all-start.1 = ((f32[8,16,1024]{2,1,0:T(8,128)}), f32[8,16,1024]{2,1,0:T(8,128)S(1)}, u32[]{:S(2)}, u32[]{:S(2)}) async-start(f32[8,16,1024]{2,1,0:T(8,128)} %broadcast_in_dim.49), calls=%async_computation.1 | async-start | bytes 1048576 | tf_op jit(solution)/shard_map/all_to_all | solution.py:13
  76.0 2.6 %abs_reduce_fusion = bf16[1024]{0:T(1024)(128)(2,1)S(1)} fusion(bf16[8,256,1024]{2,1,0:T(8,128)(2,1)} %all-to-all-done), kind=kLoop, calls=%fused_computation.5 | loop fusion | flops 4193280 | bytes 4196352 | tf_op jit(solution)/shard_map/reduce_max | solution.py:75
  78.6 7.4 %all-to-all-done.1 = f32[8,16,1024]{2,1,0:T(8,128)S(1)} async-done(((f32[8,16,1024]{2,1,0:T(8,128)}), f32[8,16,1024]{2,1,0:T(8,128)S(1)}, u32[]{:S(2)}, u32[]{:S(2)}) %all-to-all-start.1) | async-done | bytes 524320 | tf_op jit(solution)/shard_map/all_to_all | solution.py:13
  86.0 1.0 broadcast_in_dim.51
  87.1 17.3 %all-to-all-start.3 = ((f32[64,1,1708]{2,1,0:T(1,128)}), f32[64,1,1708]{2,1,0:T(1,128)}, u32[]{:S(2)}, u32[]{:S(2)}) async-start(f32[64,1,1708]{2,1,0:T(1,128)} %broadcast_in_dim.51), calls=%async_computation.3 | async-start | bytes 917504 | tf_op jit(solution)/shard_map/all_to_all | solution.py:13
  104.4 0.0 copy-done.3
  104.4 0.1 dynamic_slice.7
  104.5 30.5 %all-to-all-done.3 = f32[64,1,1708]{2,1,0:T(1,128)} async-done(((f32[64,1,1708]{2,1,0:T(1,128)}), f32[64,1,1708]{2,1,0:T(1,128)}, u32[]{:S(2)}, u32[]{:S(2)}) %all-to-all-start.3) | async-done | bytes 437280 | tf_op jit(solution)/shard_map/all_to_all | solution.py:13
  135.0 1.3 reduce_max.49
  136.3 0.0 copy-done.2
  136.4 0.6 fusion.13
  137.0 6.5 %fusion.10 = bf16[1024,684]{0,1:T(8,128)(2,1)} fusion(bf16[2048,684]{0,1:T(8,128)(2,1)S(1)} %copy-done, f32[684]{0:T(1024)S(1)} %maximum_divide_fusion, bf16[2048,1024]{1,0:T(8,128)(2,1)} %bitcast.4, f32[1024]{0:T(1024)S(1)} %maximum_divide_fusion.1), kind=kOutput, calls=%fused_computation.14 | convolution fusion | flops 2883596288 | bytes 8403632 | tf_op jit(solution)/shard_map/dot_general | solution.py:76
  143.5 2.6 %copy.11 = bf16[1024,684]{1,0:T(8,128)(2,1)} copy(bf16[1024,684]{0,1:T(8,128)(2,1)} %fusion.10) | data formatting | bytes 2801664 | tf_op jit(solution)/shard_map/convert_element_type | solution.py:80
  146.1 4.7 %all-to-all-start.2 = ((bf16[64,16,684]{2,1,0:T(8,128)(2,1)}), bf16[64,16,684]{2,1,0:T(8,128)(2,1)S(1)}, u32[]{:S(2)}, u32[]{:S(2)}) async-start(bf16[64,16,684]{2,1,0:T(8,128)(2,1)} %bitcast.2), calls=%async_computation.2 | async-start | bytes 3145728 | tf_op jit(solution)/shard_map/all_to_all | solution.py:29
  150.8 0.1 dynamic_slice.6
  150.9 0.0 slice-done
  150.9 0.6 bitcast_select_fusion
  151.5 77.9 %all-to-all-done.2 = bf16[64,16,684]{2,1,0:T(8,128)(2,1)S(1)} async-done(((bf16[64,16,684]{2,1,0:T(8,128)(2,1)}), bf16[64,16,684]{2,1,0:T(8,128)(2,1)S(1)}, u32[]{:S(2)}, u32[]{:S(2)}) %all-to-all-start.2) | async-done | bytes 1400864 | tf_op jit(solution)/shard_map/all_to_all | solution.py:29
  229.4 0.3 convert_reduce_fusion
  229.7 0.7 divide_multiply_fusion
  (13 shorter events, 0.1 us)
Async XLA Ops:
  4.2 6.3 %copy-start = (bf16[2048,684]{0,1:T(8,128)(2,1)S(1)}, bf16[2048,684]{0,1:T(8,128)(2,1)}, u32[]{:S(2)}) copy-start(bf16[2048,684]{0,1:T(8,128)(2,1)} %param.7) | copy-start | bytes 8404996
  4.2 6.9 %copy-start.4 = (s32[1024]{0:T(1024)S(1)}, s32[1024]{0:T(1024)}, u32[]{:S(2)}) copy-start(s32[1024]{0:T(1024)} %param.10) | copy-start | bytes 12292
  4.2 7.0 %copy-start.1 = (f32[1,16,1024]{2,1,0:T(8,128)S(1)}, f32[1,16,1024]{2,1,0:T(8,128)}, u32[]{:S(2)}) copy-start(f32[1,16,1024]{2,1,0:T(8,128)} %param.8) | copy-start | bytes 196612
  4.2 65.9 %all-to-all-start = ((bf16[8,256,1024]{2,1,0:T(8,128)(2,1)}), bf16[8,256,1024]{2,1,0:T(8,128)(2,1)}, u32[]{:S(2)}, u32[]{:S(2)}) async-start(bf16[8,256,1024]{2,1,0:T(8,128)(2,1)} %stack.2), calls=%async_computation | async-start | bytes 8388608 | tf_op jit(solution)/shard_map/all_to_all | solution.py:72
  11.1 93.3 %copy-start.3 = (s32[6496]{0:T(1024)S(1)}, s32[6496]{0:T(1024)}, u32[]{:S(2)}) copy-start(s32[6496]{0:T(1024)} %param.11) | copy-start | bytes 77956
  11.2 125.2 %copy-start.2 = (f32[16,684]{1,0:T(8,128)S(1)}, f32[16,684]{1,0:T(8,128)}, u32[]{:S(2)}) copy-start(f32[16,684]{1,0:T(8,128)} %param.9) | copy-start | bytes 131332
  70.9 15.1 %all-to-all-start.1 = ((f32[8,16,1024]{2,1,0:T(8,128)}), f32[8,16,1024]{2,1,0:T(8,128)S(1)}, u32[]{:S(2)}, u32[]{:S(2)}) async-start(f32[8,16,1024]{2,1,0:T(8,128)} %broadcast_in_dim.49), calls=%async_computation.1 | async-start | bytes 1048576 | tf_op jit(solution)/shard_map/all_to_all | solution.py:13
  87.1 48.0 %all-to-all-start.3 = ((f32[64,1,1708]{2,1,0:T(1,128)}), f32[64,1,1708]{2,1,0:T(1,128)}, u32[]{:S(2)}, u32[]{:S(2)}) async-start(f32[64,1,1708]{2,1,0:T(1,128)} %broadcast_in_dim.51), calls=%async_computation.3 | async-start | bytes 917504 | tf_op jit(solution)/shard_map/all_to_all | solution.py:13
  143.5 7.4 %slice-start = ((s32[6496]{0:T(1024)}), s32[1024]{0:T(1024)S(1)}, s32[]{:S(2)}) async-start(s32[6496]{0:T(1024)} %param.11), calls=%async_computation.4 | async-start | bytes 8192 | tf_op jit(solution)/shard_map/slice | solution.py:85
  146.1 83.3 %all-to-all-start.2 = ((bf16[64,16,684]{2,1,0:T(8,128)(2,1)}), bf16[64,16,684]{2,1,0:T(8,128)(2,1)S(1)}, u32[]{:S(2)}, u32[]{:S(2)}) async-start(bf16[64,16,684]{2,1,0:T(8,128)(2,1)} %bitcast.2), calls=%async_computation.2 | async-start | bytes 3145728 | tf_op jit(solution)/shard_map/all_to_all | solution.py:29
